TPU v7x, 32 devices: a whole 2x2x4 slice. The times are simulated.
32 devices in a mesh: section: 4 (over z), mp: 4 (over y, core), dp: 2 (over x).
Axes of the slice: x: 2, y: 2, z: 4, core: 2. Of those that a mesh axis runs over, the one named last changes fastest.
Arguments:
- context: bfloat16 [4, 1024, 6144], P('section', None, 'mp'), may hold values from -6 to 6
- out_weight: bfloat16 [4, 6144, 4, 2, 1536], P('section', 'mp', None, 'dp'), may hold values from -0.078125 to 0.078125
- residual: bfloat16 [4, 1024, 12288], P('section', None, ('mp', 'dp')), may hold values from -6 to 6
- layer_norm_gain: float32 [4, 12288], P('section', 'mp'), may hold values from 0.25 to 1.75
- layer_norm_bias: float32 [4, 12288], P('section', 'mp'), may hold values from -3 to 3
- ln_cotangent: bfloat16 [4, 1024, 12288], P('section', 'dp', 'mp'), may hold values from -6 to 6
Outputs:
- layer_norm_output: bfloat16 [4, 1024, 12288], P('section', 'dp', 'mp')
- resid_grad: bfloat16 [4, 1024, 12288], P('section', 'dp', 'mp')
All inputs are finite; a program needn't handle non-finite values.
Results may differ from a plain program's by a relative error of at most 0.0047.
Values may be sent and summed in bfloat16 or wider, within the bound.
A program may use at most 128 MiB of HBM per device.

v0:
```python
import jax
import jax.numpy as jnp
from jax import lax
from jax.sharding import PartitionSpec as P

D = 12288


epsilon = 1e-05


def passed_along(x, axis, by):
    devices = lax.axis_size(axis)
    return lax.ppermute(x, axis, [(i, (i + by) % devices) for i in range(devices)])


def cross_section(values):
    return passed_along(values, "section", 1)


def relayout(values):
    return lax.all_to_all(values, "dp", split_axis=0, concat_axis=1, tiled=True)


def local(context, out_weight, residual, layer_norm_gain, layer_norm_bias, ln_cotangent):
    local_ctx = context[0]
    weights = out_weight[0]
    weights = weights.reshape(weights.shape[0], weights.shape[1], weights.shape[3])
    summed = lax.psum_scatter(
        jnp.einsum("th,hjr->jtr", local_ctx, weights, preferred_element_type=jnp.float32),
        "mp",
        scatter_dimension=0,
        tiled=True,
    )
    section_out = (residual[0].astype(jnp.float32) + summed[0]).astype(jnp.bfloat16)
    arrived = relayout(cross_section(section_out))
    arrived = arrived.astype(jnp.float32)
    norm_gain_row = layer_norm_gain[0][None, :]
    gain_scaled = ln_cotangent[0].astype(jnp.float32) * norm_gain_row
    width = float(D)
    sum_one, sum_two, sum_three, sum_four = lax.psum(
        (
            jnp.sum(arrived, axis=-1, keepdims=True),
            jnp.sum(arrived * arrived, axis=-1, keepdims=True),
            jnp.sum(gain_scaled, axis=-1, keepdims=True),
            jnp.sum(gain_scaled * arrived, axis=-1, keepdims=True),
        ),
        "mp",
    )
    average = sum_one / width
    variance = sum_two / width - average * average
    inverse_deviation = lax.rsqrt(variance + epsilon)
    normalized_input = (arrived - average) * inverse_deviation
    input_mean = sum_three / width
    squared_mean = inverse_deviation * (sum_four / width - average * input_mean)
    layer_norm_output = (normalized_input * norm_gain_row + layer_norm_bias[0][None, :]).astype(
        jnp.bfloat16
    )
    incoming_gradient = (
        inverse_deviation * (gain_scaled - input_mean - normalized_input * squared_mean)
    ).astype(jnp.bfloat16)
    returned = passed_along(incoming_gradient, "section", -1)
    return (layer_norm_output[None], returned[None])


def solution(mesh):
    in_specs = (
        P("section", None, "mp"),
        P("section", "mp", None, "dp", None),
        P("section", None, ("mp", "dp")),
        P("section", "mp"),
        P("section", "mp"),
        P("section", "dp", "mp"),
    )
    out_specs = (P("section", "dp", "mp"), P("section", "dp", "mp"))
    return jax.shard_map(local, mesh=mesh, in_specs=in_specs, out_specs=out_specs, check_vma=False)
```

profile of v0, /device:TPU:0, one launch (start us, length us, event | category | flops | bytes accessed | tf_op | source)
XLA Modules:
  0.0 442.0 jit_solution(2496322216225081328)
XLA Ops:
  7.2 0.0 copy-start
  7.2 0.0 reduce-scatter.2.cloned.1.call-start
  7.2 1.8 copy-done
  9.1 25.8 %fusion.2 = f32[4,1024,1536]{1,2,0:T(8,128)} fusion(bf16[1536,4,1536]{2,1,0:T(4,128)(2,1)} %bitcast.52, bf16[1,1024,1536]{2,1,0:T(8,128)(2,1)S(1)} %copy-done), kind=kOutput, calls=%fused_computation.2 | convolution fusion | flops 19327352832 | bytes 47185920 | tf_op jit(solution)/shard_map/th,hjr->jtr/dot_general | solution.py:30
  34.9 0.0 reduce-scatter.2.cloned.1.call-update
  34.9 3.2 copy.16
  38.1 181.6 %reduce-scatter.2.cloned.1.call-done = f32[1,1024,1536]{1,2,0:T(8,128)} async-done(((f32[4,1024,1536]{1,2,0:T(8,128)}), f32[1,1024,1536]{1,2,0:T(8,128)}) %reduce-scatter.2.cloned.1.call-update) | async-done | bytes 6291472 | tf_op jit(solution)/shard_map/reduce_scatter | solution.py:29
  219.7 4.0 fusion.12
  223.6 1.5 collective-permute-start
  225.2 70.0 %collective-permute-done = bf16[1024,1536]{0,1:T(8,128)(2,1)S(1)} collective-permute-done((bf16[1024,1536]{0,1:T(8,128)(2,1)S(1)}, bf16[1024,1536]{0,1:T(8,128)(2,1)S(1)}, u32[]{:S(2)}, u32[]{:S(2)}) %collective-permute-start) | collective-permute-done | bytes 3145760 | tf_op jit(solution)/shard_map/ppermute | solution.py:14
  295.2 0.2 copy.28
  295.4 38.0 %all_to_all.13 = bf16[2,512,1536]{1,2,0:T(8,128)(2,1)S(1)} all-to-all(bf16[2,512,1536]{1,2,0:T(8,128)(2,1)S(1)} %bitcast.36), channel_id=1, replica_groups=mesh['section'=4,'mp'=4,'dp'=2] {'dp'}, dimensions={0} | all-to-all | bytes 6291456 | tf_op jit(solution)/shard_map/all_to_all | solution.py:22
  333.4 3.6 convert_element_type.72
  336.9 6.5 %copy.20 = f32[512,3072]{1,0:T(8,128)} copy(f32[512,3072]{0,1:T(8,128)} %bitcast.34) | data formatting | bytes 12582912 | tf_op jit(solution)/shard_map/convert_element_type | solution.py:37
  343.5 0.0 copy-done.2
  343.5 5.0 %fusion.7 = (f32[512]{0:T(512)S(1)}, f32[512]{0:T(512)S(1)}) fusion(bf16[1,512,3072]{2,1,0:T(8,128)(2,1)} %param.11, f32[3072]{0:T(1024)S(1)} %bitcast.38, f32[512,3072]{1,0:T(8,128)} %copy.20), kind=kLoop, calls=%fused_computation.6 | loop fusion | flops 7863296 | bytes 9453568 | tf_op jit(solution)/shard_map/reduce_sum | solution.py:45
  348.4 0.9 convert_reduce_fusion
  349.3 5.7 %all-reduce = (f32[512,1]{0,1:T(1,128)S(1)}, f32[512,1]{0,1:T(1,128)S(1)}, f32[512,1]{0,1:T(1,128)S(1)}, f32[512,1]{0,1:T(1,128)S(1)}) all-reduce(f32[512,1]{0,1:T(1,128)S(1)} %bitcast.49, f32[512,1]{0,1:T(1,128)S(1)} %bitcast.48, f32[512,1]{0,1:T(1,128)S(1)} %bitcast.47, ...), channel_id=1, replica_groups=mesh['section'=4,'mp'=4,'dp'=2] {'mp'}, use_global_device_ids=true, to_apply=%region_4.0 | all-reduce | flops 2048 | bytes 16384 | tf_op jit(solution)/shard_map/psum | solution.py:41
  355.1 6.2 %fusion.10 = bf16[512,3072]{1,0:T(8,128)(2,1)} fusion(f32[512,3072]{1,0:T(8,128)} %copy.20, bf16[1,512,3072]{2,1,0:T(8,128)(2,1)} %param.11, f32[512]{0:T(512)S(1)} %bitcast.50, f32[512]{0:T(512)S(1)} %bitcast.43, f32[512]{0:T(512)S(1)} %bitcast.51, f32[3072]{0:T(1024)S(1)} %bitcast.39, f32[512]{0:T(512)S(1)} %bitcast.41), kind=kLoop, calls=%fused_computation.9 | loop fusion | flops 14155776 | bytes 12603392 | tf_op jit(solution)/shard_map/convert_element_type | solution.py:61
  361.2 1.8 collective-permute-start.1
  363.1 6.5 %copy.19 = f32[1,512,3072]{2,1,0:T(8,128)} copy(f32[1,512,3072]{1,2,0:T(8,128)} %bitcast.35) | data formatting | bytes 12582912 | tf_op jit(solution)/shard_map/convert_element_type | solution.py:37
  369.6 6.1 %add_convert_fusion = bf16[1,512,3072]{2,1,0:T(8,128)(2,1)} fusion(f32[1,512,3072]{2,1,0:T(8,128)} %copy.19, f32[3072]{0:T(1024)S(1)} %bitcast.45, f32[3072]{0:T(1024)S(1)} %bitcast.40, f32[512]{0:T(512)S(1)} %bitcast.42, f32[512]{0:T(512)S(1)} %bitcast.44), kind=kLoop, calls=%fused_computation.11 | loop fusion | flops 7864320 | bytes 9465856 | tf_op jit(solution)/shard_map/convert_element_type | solution.py:56
  375.7 55.7 %collective-permute-done.1 = bf16[512,3072]{1,0:T(8,128)(2,1)} collective-permute-done((bf16[512,3072]{1,0:T(8,128)(2,1)}, bf16[512,3072]{1,0:T(8,128)(2,1)}, u32[]{:S(2)}, u32[]{:S(2)}) %collective-permute-start.1) | collective-permute-done | bytes 3145760 | tf_op jit(solution)/shard_map/ppermute | solution.py:14
  431.4 3.8 copy.30
  (6 shorter events, 0.0 us)
Async XLA Ops:
  7.2 1.9 copy-start
  7.2 212.5 %reduce-scatter.2.cloned.1.call-start = ((), (), s32[]{:S(2)}) async-start(), calls=%async_computation.2 | async-start | bytes 31457280 | tf_op jit(solution)/shard_map/reduce_scatter | solution.py:29
  223.6 71.5 %collective-permute-start = (bf16[1024,1536]{0,1:T(8,128)(2,1)S(1)}, bf16[1024,1536]{0,1:T(8,128)(2,1)S(1)}, u32[]{:S(2)}, u32[]{:S(2)}) collective-permute-start(bf16[1024,1536]{0,1:T(8,128)(2,1)S(1)} %fusion.12), channel_id=1, source_target_pairs={{0,8},{8,16},{16,24},{24,0},{1,9},{9,17},{17,25},{25,1},{2,10},{10... | collective-permute-start | bytes 9437192 | tf_op jit(solution)/shard_map/ppermute | solution.py:14
  336.9 6.5 %copy-start.2 = (f32[1,3072]{1,0:T(1,128)S(1)}, f32[1,3072]{1,0:T(1,128)}, u32[]{:S(2)}) copy-start(f32[1,3072]{1,0:T(1,128)} %param.9) | copy-start | bytes 36868
  361.2 70.1 %collective-permute-start.1 = (bf16[512,3072]{1,0:T(8,128)(2,1)}, bf16[512,3072]{1,0:T(8,128)(2,1)}, u32[]{:S(2)}, u32[]{:S(2)}) collective-permute-start(bf16[512,3072]{1,0:T(8,128)(2,1)} %fusion.10), channel_id=1, source_target_pairs={{0,24},{8,0},{16,8},{24,16},{1,25},{9,1},{17,9},{25,17},{2,26},{10... | collective-permute-start | bytes 9437192 | tf_op jit(solution)/shard_map/ppermute | solution.py:14
  363.1 6.5 %copy-start.3 = (f32[1,3072]{1,0:T(1,128)S(1)}, f32[1,3072]{1,0:T(1,128)}, u32[]{:S(2)}) copy-start(f32[1,3072]{1,0:T(1,128)} %param.10) | copy-start | bytes 36868
  369.6 65.5 %copy-start.1 = (bf16[1,1024,1536]{2,1,0:T(8,128)(2,1)S(1)}, bf16[1,1024,1536]{2,1,0:T(8,128)(2,1)}, u32[]{:S(2)}) copy-start(bf16[1,1024,1536]{2,1,0:T(8,128)(2,1)} %param.6) | copy-start | bytes 9437188
Sparse Core Ops, SparseCore 0:
  35.0 184.6 reduce-scatter.1
where the time goes:
time: 442 us
  waiting for transfers between devices  307 us (69%)
  blocking collectives  43.7 us (10%)
  matrix products  25.8 us (6%)
  other arithmetic  25.6 us (6%)
  local copies, waits for them, and re-layouts  22.1 us (5%)
  between operations  14.1 us (3%)
    reduce_scatter x1, waiting for transfers between devices, local(): lax.psum_scatter(jnp.einsum('th,hjr->jtr', local_ctx, weights, preferred_...  182 us
    ppermute x2, waiting for transfers between devices, passed_along(): lax.ppermute(x, axis, [(i, (i + by) % devices) for i in range(devices)])  126 us
    all_to_all x1, blocking collectives, relayout(): return lax.all_to_all(values, 'dp', split_axis=0, concat_axis=1, tiled=True)  38 us
    dot_general x1, matrix products, local(): jnp.einsum('th,hjr->jtr', local_ctx, weights, preferred_element_type=jnp....  25.8 us
    convert_element_type x2, local copies, waits for them, and re-layouts, local(): arrived = arrived.astype(jnp.float32)  13.1 us
  transfers between devices with their start and end apart: 3, of which 3 were waited for; matrix products, arithmetic and copies ran while one was open for 4% of the time, Pallas kernels for 0%

commit v1 on v0

v1 whole, which is shorter than its diff:
```python
import jax
import jax.numpy as jnp
from jax import lax
from jax.sharding import PartitionSpec as P


epsilon = 1e-05
CHUNKS = 4


def passed_along(x, axis, by):
    devices = lax.axis_size(axis)
    return lax.ppermute(x, axis, [(i, (i + by) % devices) for i in range(devices)])


def pick(x, index, axis=0):
    return lax.dynamic_index_in_dim(x, index, axis, keepdims=False)


def head_sum(part):
    n_mp = lax.axis_size("mp")
    me = lax.axis_index("mp")
    groups, core, group = n_mp // 2, me % 2, me // 2
    pairs = part.reshape(groups, 2, *part.shape[1:])
    away = pick(pairs, 1 - core, 1).astype(jnp.bfloat16)
    near = lax.ppermute(away, "mp", [(i, i ^ 1) for i in range(n_mp)])
    both = pick(pairs, core, 1) + near.astype(jnp.float32)
    total = pick(both, group)
    for k in range(1, groups):
        send = pick(both, (group + k) % groups).astype(jnp.bfloat16)
        got = lax.ppermute(
            send, "mp", [(i, ((i // 2 + k) % groups) * 2 + i % 2) for i in range(n_mp)]
        )
        total = total + got.astype(jnp.float32)
    return total


def relayout(values):
    n_dp, _, _ = values.shape
    if n_dp != 2:
        out = lax.all_to_all(values, "dp", split_axis=0, concat_axis=2, tiled=True)
        return out[0]
    me = lax.axis_index("dp")
    own = pick(values, me)
    got = lax.ppermute(pick(values, 1 - me), "dp", [(0, 1), (1, 0)])
    first = me == 0
    return jnp.concatenate([jnp.where(first, own, got), jnp.where(first, got, own)], axis=1)


def local(context, out_weight, residual, layer_norm_gain, layer_norm_bias, ln_cotangent):
    n_dp = lax.axis_size("dp")
    n_mp = lax.axis_size("mp")
    cotangent = passed_along(ln_cotangent[0], "section", -1)
    next_gain = passed_along(layer_norm_gain, "section", -1)
    weights = out_weight[0]
    weights = weights.reshape(weights.shape[0], weights.shape[1], weights.shape[3])
    tokens, heads = context.shape[1:]
    features = weights.shape[2]
    per = tokens // n_dp // CHUNKS
    local_ctx = context[0].reshape(n_dp, CHUNKS, per, heads)
    local_res = residual[0].reshape(n_dp, CHUNKS, per, features)

    blocks, arrived = [], []
    for c in range(CHUNKS):
        rows = local_ctx[:, c].reshape(n_dp * per, heads)
        part = jnp.einsum("th,hjr->jtr", rows, weights, preferred_element_type=jnp.float32)
        summed = head_sum(part)
        res = local_res[:, c].reshape(n_dp * per, features)
        section_out = (res.astype(jnp.float32) + summed).astype(jnp.bfloat16)
        block = relayout(section_out.reshape(n_dp, per, features))
        blocks.append(block)
        arrived.append(passed_along(block, "section", 1))

    width = float(n_mp * n_dp * features)
    sums = []
    for c in range(CHUNKS):
        x = blocks[c].astype(jnp.float32)
        g = cotangent[c * per:(c + 1) * per].astype(jnp.float32) * next_gain
        sums.append(
            jnp.stack([jnp.sum(x, -1), jnp.sum(x * x, -1), jnp.sum(g, -1), jnp.sum(g * x, -1)])
        )
    sums = lax.psum(jnp.concatenate(sums, axis=1), "mp")
    average = sums[0] / width
    variance = sums[1] / width - average * average
    inverse_deviation = lax.rsqrt(variance + epsilon)
    input_mean = sums[2] / width
    squared_mean = inverse_deviation * (sums[3] / width - average * input_mean)
    there = passed_along(jnp.stack([average, inverse_deviation]), "section", 1)

    grads, outs = [], []
    for c in range(CHUNKS):
        rows = slice(c * per, (c + 1) * per)
        x = blocks[c].astype(jnp.float32)
        g = cotangent[rows].astype(jnp.float32) * next_gain
        rstd = inverse_deviation[rows][:, None]
        xhat = (x - average[rows][:, None]) * rstd
        grads.append(
            (rstd * (g - input_mean[rows][:, None] - xhat * squared_mean[rows][:, None])).astype(
                jnp.bfloat16
            )
        )
        y = arrived[c].astype(jnp.float32)
        yhat = (y - there[0, rows][:, None]) * there[1, rows][:, None]
        outs.append((yhat * layer_norm_gain + layer_norm_bias).astype(jnp.bfloat16))
    return (jnp.concatenate(outs)[None], jnp.concatenate(grads)[None])


def solution(mesh):
    in_specs = (
        P("section", None, "mp"),
        P("section", "mp", None, "dp", None),
        P("section", None, ("mp", "dp")),
        P("section", "mp"),
        P("section", "mp"),
        P("section", "dp", "mp"),
    )
    out_specs = (P("section", "dp", "mp"), P("section", "dp", "mp"))
    return jax.shard_map(local, mesh=mesh, in_specs=in_specs, out_specs=out_specs, check_vma=False)
```

time: 442 us -> 224 us (0.51)
  waiting for transfers between devices: 307 us -> 103 us
  blocking collectives: 43.7 us -> 6.84 us
  starting transfers between devices: 3.4 us -> 21.7 us
  matrix products: 25.8 us -> 40.3 us
  between operations: 14.1 us -> 1.17 us
  other arithmetic: 25.6 us -> 31.2 us
    reduce_scatter x1 -> x0, waiting for transfers between devices: 182 us -> none  [local(): lax.psum_scatter(jnp.einsum('th,hjr->jtr', local_ctx, weights, preferred_...]
    ppermute x2 -> x7, waiting for transfers between devices: 126 us -> 39.4 us  [passed_along(): lax.ppermute(x, axis, [(i, (i + by) % devices) for i in range(devices)])]
    ppermute x0 -> x12, waiting for transfers between devices: none -> 64 us  [the longest x4 53.7 us: head_sum(): lax.ppermute(send, 'mp', [(i, (i // 2 + k) % groups * 2 + i % 2) for i in...]
    all_to_all x1 -> x0, blocking collectives: 38 us -> none  [relayout(): return lax.all_to_all(values, 'dp', split_axis=0, concat_axis=1, tiled=True)]
    dot_general x1 -> x4, matrix products: 25.8 us -> 40.3 us  [local(): jnp.einsum('th,hjr->jtr', rows, weights, preferred_element_type=jnp.float32)]
    ppermute x0 -> x12, starting transfers between devices: none -> 11.3 us  [the longest x4 5.26 us: head_sum(): lax.ppermute(send, 'mp', [(i, (i // 2 + k) % groups * 2 + i % 2) for i in...]
    convert_element_type x4 -> x7, other arithmetic: 19.7 us -> 9.34 us  [the longest x2 4.24 us: local(): (rstd * (g - input_mean[rows][:, None] - xhat * squared_mean[rows][:, Non...]
    add x0 -> x4, other arithmetic: none -> 9 us  [head_sum(): both = pick(pairs, core, 1) + near.astype(jnp.float32)]
  transfers between devices with their start and end apart: 3 -> 19, of which waited for: 3 -> 7; matrix products, arithmetic and copies ran while one was open for 4% -> 28% of each run, Pallas kernels for 0% -> 0%
where the time goes in v1:
time: 224 us
  waiting for transfers between devices  103 us (46%)
  matrix products  40.3 us (18%)
  other arithmetic  31.2 us (14%)
  starting transfers between devices  21.7 us (10%)
  local copies, waits for them, and re-layouts  18.9 us (8%)
  blocking collectives  6.84 us (3%)
    ppermute x4, waiting for transfers between devices, head_sum(): lax.ppermute(send, 'mp', [(i, (i // 2 + k) % groups * 2 + i % 2) for i in...  53.7 us
    dot_general x4, matrix products, local(): jnp.einsum('th,hjr->jtr', rows, weights, preferred_element_type=jnp.float32)  40.3 us
    ppermute x7, waiting for transfers between devices, passed_along(): lax.ppermute(x, axis, [(i, (i + by) % devices) for i in range(devices)])  39.4 us
    convert_element_type x4, local copies, waits for them, and re-layouts, head_sum(): away = pick(pairs, 1 - core, 1).astype(jnp.bfloat16)  12.8 us
    ppermute x7, starting transfers between devices, passed_along(): lax.ppermute(x, axis, [(i, (i + by) % devices) for i in range(devices)])  10.4 us
    ppermute x4, waiting for transfers between devices, relayout(): got = lax.ppermute(pick(values, 1 - me), 'dp', [(0, 1), (1, 0)])  10.4 us
    add x4, other arithmetic, head_sum(): both = pick(pairs, core, 1) + near.astype(jnp.float32)  9 us
    psum x1, blocking collectives, local(): sums = lax.psum(jnp.concatenate(sums, axis=1), 'mp')  6.84 us
  transfers between devices with their start and end apart: 19, of which 7 were waited for; matrix products, arithmetic and copies ran while one was open for 28% of the time, Pallas kernels for 0%

profile of v1, /device:TPU:0, one launch (start us, length us, event | category | flops | bytes accessed | tf_op | source)
XLA Modules:
  0.0 223.6 jit_solution(7371059936392357764)
XLA Ops:
  0.6 3.3 %fusion.56 = (bf16[2,1,128,1536]{3,2,1,0:T(8,128)(2,1)S(1)}, bf16[2,1,128,1536]{3,2,1,0:T(8,128)(2,1)S(1)}, bf16[2,1,128,1536]{3,2,1,0:T(8,128)(2,1)}, bf16[2,1,128,1536]{3,2,1,0:T(8,128)(2,1)}) fusion(bf16[2,4,128,1536]{3,2,1,0:T(8,128)(2,1)} %bitcast.207), kind=kLoop, calls=%fused_computation.149 | loop fusion | bytes 6291456 | tf_op jit(solution)/shard_map/slice | solution.py:65
  4.0 15.2 %fusion.6 = f32[4,1536,256]{1,2,0:T(8,128)} fusion(bf16[256,1536,1]{1,0,2:T(8,128)(2,1)} %bitcast.220, bf16[1536,4,1536]{2,1,0:T(4,128)(2,1)} %bitcast.187), kind=kOutput, calls=%fused_computation.6 | convolution fusion | flops 4831838208 | bytes 25952256 | tf_op jit(solution)/shard_map/th,hjr->jtr/dot_general | solution.py:66
  19.1 3.2 %fusion.39 = bf16[2,256,1536]{2,1,0:T(8,128)(2,1)} fusion(f32[2,2,256,1536]{3,2,1,0:T(8,128)} %bitcast.205, s32[]{:T(128)S(6)} %select_n.108), kind=kLoop, calls=%fused_computation.65 | loop fusion | bytes 3145732 | tf_op jit(solution)/shard_map/convert_element_type | solution.py:25
  22.9 8.9 %fusion.2 = f32[4,1536,256]{1,2,0:T(8,128)} fusion(bf16[256,1536,1]{1,0,2:T(8,128)(2,1)} %bitcast.219, bf16[1536,4,1536]{2,1,0:T(4,128)(2,1)S(1)} %bitcast.190), kind=kOutput, calls=%fused_computation.2 | convolution fusion | flops 4831838208 | bytes 25952256 | tf_op jit(solution)/shard_map/th,hjr->jtr/dot_general | solution.py:66
  31.7 3.2 %fusion.37 = bf16[2,256,1536]{2,1,0:T(8,128)(2,1)} fusion(f32[2,2,256,1536]{3,2,1,0:T(8,128)} %bitcast.201, s32[]{:T(128)S(6)} %select_n.108), kind=kLoop, calls=%fused_computation.63 | loop fusion | bytes 3145732 | tf_op jit(solution)/shard_map/convert_element_type | solution.py:25
  35.0 8.1 %fusion.4 = f32[4,1536,256]{1,2,0:T(8,128)} fusion(bf16[256,1536,1]{1,0,2:T(8,128)(2,1)S(1)} %bitcast.218, bf16[1536,4,1536]{2,1,0:T(4,128)(2,1)S(1)} %bitcast.191), kind=kOutput, calls=%fused_computation.4 | convolution fusion | flops 4831838208 | bytes 25952256 | tf_op jit(solution)/shard_map/th,hjr->jtr/dot_general | solution.py:66
  43.1 3.2 %fusion.38 = bf16[2,256,1536]{2,1,0:T(8,128)(2,1)} fusion(f32[2,2,256,1536]{3,2,1,0:T(8,128)} %bitcast.197, s32[]{:T(128)S(6)} %select_n.108), kind=kLoop, calls=%fused_computation.64 | loop fusion | bytes 3145732 | tf_op jit(solution)/shard_map/convert_element_type | solution.py:25
  46.8 8.2 %fusion = f32[4,1536,256]{1,2,0:T(8,128)} fusion(bf16[256,1536,1]{1,0,2:T(8,128)(2,1)S(1)} %bitcast.217, bf16[1536,4,1536]{2,1,0:T(4,128)(2,1)S(1)} %bitcast.192), kind=kOutput, calls=%fused_computation | convolution fusion | flops 4831838208 | bytes 25952256 | tf_op jit(solution)/shard_map/th,hjr->jtr/dot_general | solution.py:66
  54.9 3.2 %fusion.36 = bf16[2,256,1536]{2,1,0:T(8,128)(2,1)} fusion(f32[2,2,256,1536]{3,2,1,0:T(8,128)} %bitcast.193, s32[]{:T(128)S(6)} %select_n.108), kind=kLoop, calls=%fused_computation.62 | loop fusion | bytes 3145732 | tf_op jit(solution)/shard_map/convert_element_type | solution.py:25
  58.1 5.1 %collective-permute-start.4 = (bf16[512,3072]{1,0:T(8,128)(2,1)}, bf16[512,3072]{1,0:T(8,128)(2,1)S(1)}, u32[]{:S(2)}, u32[]{:S(2)}) collective-permute-start(bf16[512,3072]{1,0:T(8,128)(2,1)} %bitcast.18), channel_id=1, source_target_pairs={{0,24},{8,0},{16,8},{24,16},{1,25},{9,1},{17,9},{25,17},{2,26},{10... | collective-permute-start | bytes 9437192 | tf_op jit(solution)/shard_map/ppermute | solution.py:13
  63.2 2.2 fusion.55
  66.0 3.0 %bitcast_add_fusion = f32[2,256,1536]{2,1,0:T(8,128)S(1)} fusion(bf16[2,256,1536]{2,1,0:T(8,128)(2,1)} %collective-permute-done.12, f32[2,2,256,1536]{3,2,1,0:T(8,128)} %bitcast.206, s32[]{:T(128)S(6)} %select_n.107), kind=kLoop, calls=%fused_computation.10 | loop fusion | flops 1572864 | bytes 7864324 | tf_op jit(solution)/shard_map/add | solution.py:27
  70.7 2.1 bitcast_add_fusion.2
  79.2 10.4 %collective-permute-done.13 = bf16[256,1536]{1,0:T(8,128)(2,1)S(1)} collective-permute-done((bf16[256,1536]{1,0:T(8,128)(2,1)S(1)}, bf16[256,1536]{1,0:T(8,128)(2,1)S(1)}, u32[]{:S(2)}, u32[]{:S(2)}) %collective-permute-start.13) | collective-permute-done | bytes 786464 | tf_op jit(solution)/shard_map/ppermute | solution.py:31
  91.5 14.9 %collective-permute-done.7 = bf16[256,1536]{1,0:T(8,128)(2,1)S(1)} collective-permute-done((bf16[256,1536]{1,0:T(8,128)(2,1)S(1)}, bf16[256,1536]{1,0:T(8,128)(2,1)S(1)}, u32[]{:S(2)}, u32[]{:S(2)}) %collective-permute-start.7) | collective-permute-done | bytes 786464 | tf_op jit(solution)/shard_map/ppermute | solution.py:31
  108.3 14.9 %collective-permute-done.10 = bf16[256,1536]{1,0:T(8,128)(2,1)S(1)} collective-permute-done((bf16[256,1536]{1,0:T(8,128)(2,1)S(1)}, bf16[256,1536]{1,0:T(8,128)(2,1)S(1)}, u32[]{:S(2)}, u32[]{:S(2)}) %collective-permute-start.10) | collective-permute-done | bytes 786464 | tf_op jit(solution)/shard_map/ppermute | solution.py:31
  125.2 13.4 %collective-permute-done.1 = bf16[256,1536]{1,0:T(8,128)(2,1)S(1)} collective-permute-done((bf16[256,1536]{1,0:T(8,128)(2,1)S(1)}, bf16[256,1536]{1,0:T(8,128)(2,1)S(1)}, u32[]{:S(2)}, u32[]{:S(2)}) %collective-permute-start.1) | collective-permute-done | bytes 786464 | tf_op jit(solution)/shard_map/ppermute | solution.py:31
  142.2 8.4 %collective-permute-done.11 = bf16[128,1536]{1,0:T(8,128)(2,1)S(1)} collective-permute-done((bf16[128,1536]{1,0:T(8,128)(2,1)S(1)}, bf16[128,1536]{1,0:T(8,128)(2,1)S(1)}, u32[]{:S(2)}, u32[]{:S(2)}) %collective-permute-start.11) | collective-permute-done | bytes 393248 | tf_op jit(solution)/shard_map/ppermute | solution.py:45
  154.7 2.0 collective-permute-done.2
  159.4 3.1 %fusion.47 = (f32[128]{0:T(128)S(1)}, f32[128]{0:T(128)S(1)}, f32[128]{0:T(128)S(1)}, f32[128]{0:T(128)S(1)}, f32[128]{0:T(128)S(1)}, /*index=5*/f32[128]{0:T(12...) fusion(f32[3072]{0:T(1024)S(1)} %bitcast.221, ...), kind=kLoop, calls=%fused_computation.92 | loop fusion | flops 17692928 | bytes 6310912 | tf_op jit(solution)/shard_map/reduce_sum | solution.py:80
  163.2 6.8 %psum.7 = f32[4,512]{1,0:T(4,128)} all-reduce(f32[4,512]{1,0:T(4,128)} %maximum_maximum_fusion), channel_id=1, replica_groups=mesh['section'=4,'mp'=4,'dp'=2] {'mp'}, use_global_device_ids=true, to_apply=%region_16.17 | all-reduce | flops 2048 | bytes 16384 | tf_op jit(solution)/shard_map/psum | solution.py:82
  172.6 2.8 %fusion.14 = (bf16[128,3072]{1,0:T(8,128)(2,1)S(1)}, bf16[128,3072]{1,0:T(8,128)(2,1)S(1)}) fusion(f32[128]{0:T(128)S(1)} %get-tuple-element.70, f32[128]{0:T(128)S(1)} %get-tuple-element.77, f32[128]{0:T(128)S(1)} %get-tuple-element.62, f32[128]{0:T(128)S(1)} %get-tuple-element.81, f32[3072]{0:T(1024)S(1)} %bitcast.222, ...), kind=kLoop, calls=%fused_computation.40 | loop fusion | flops 10223616 | bytes 4734976 | tf_op jit(solution)/shard_map/convert_element_type | solution.py:98
  178.7 39.4 %collective-permute-done.15 = f32[2,512]{1,0:T(2,128)S(1)} collective-permute-done((f32[2,512]{1,0:T(2,128)S(1)}, f32[2,512]{1,0:T(2,128)S(1)}, u32[]{:S(2)}, u32[]{:S(2)}) %collective-permute-start.15) | collective-permute-done | bytes 4128 | tf_op jit(solution)/shard_map/ppermute | solution.py:13
  218.2 3.6 %add_convert_fusion.3 = (bf16[128,3072]{1,0:T(8,128)(2,1)S(1)}, bf16[128,3072]{1,0:T(8,128)(2,1)S(1)}, bf16[128,3072]{1,0:T(8,128)(2,1)S(1)}, bf16[128,3072]{1,0:T(8,128)(2,1)S(1)}) fusion(bf16[128,3072]{1,0:T(8,128)(2,1)} %collective-permute-done.3, f32[3072]{0:T(1024)S(1)} %bitcast.224, f32[3072]{0:T(1024)S(1)} %bitcast.225, f32[128]{0:T(128)S(1)} %get-tuple-element.57, ...), kind=kLoop, calls=%fused_computation.81 | loop fusion | flops 9437184 | bytes 6320128 | tf_op jit(solution)/shard_map/convert_element_type | solution.py:104
  (114 shorter events, 33.9 us)
Async XLA Ops:
  3.9 18.9 %slice-start = ((s8[18874368]{0:T(1024)(128)(4,1)}), s8[4194304]{0:T(1024)(128)(4,1)S(1)}, s32[]{:S(2)}) async-start(s8[18874368]{0:T(1024)(128)(4,1)} %bitcast.188), calls=%async_computation | async-start | bytes 8388608
  3.9 18.9 %slice-start.1 = ((s8[18874368]{0:T(1024)(128)(4,1)}), s8[4194304]{0:T(1024)(128)(4,1)S(1)}, s32[]{:S(2)}) async-start(s8[18874368]{0:T(1024)(128)(4,1)} %bitcast.188), calls=%async_computation.1 | async-start | bytes 8388608
  3.9 18.9 %slice-start.2 = ((s8[18874368]{0:T(1024)(128)(4,1)}), s8[4194304]{0:T(1024)(128)(4,1)S(1)}, s32[]{:S(2)}) async-start(s8[18874368]{0:T(1024)(128)(4,1)} %bitcast.188), calls=%async_computation.2 | async-start | bytes 8388608
  22.3 43.1 %collective-permute-start.12 = (bf16[2,256,1536]{2,1,0:T(8,128)(2,1)}, bf16[2,256,1536]{2,1,0:T(8,128)(2,1)}, u32[]{:S(2)}, u32[]{:S(2)}) collective-permute-start(bf16[2,256,1536]{2,1,0:T(8,128)(2,1)} %fusion.39), channel_id=1, source_target_pairs={{0,2},{2,0},{4,6},{6,4},{1,3},{3,1},{5,7},{7,5},{8,10},{10,8},{12,... | collective-permute-start | bytes 4718600 | tf_op jit(solution)/shard_map/ppermute | solution.py:26
  35.0 34.1 %collective-permute-start.6 = (bf16[2,256,1536]{2,1,0:T(8,128)(2,1)}, bf16[2,256,1536]{2,1,0:T(8,128)(2,1)}, u32[]{:S(2)}, u32[]{:S(2)}) collective-permute-start(bf16[2,256,1536]{2,1,0:T(8,128)(2,1)} %fusion.37), channel_id=1, source_target_pairs={{0,2},{2,0},{4,6},{6,4},{1,3},{3,1},{5,7},{7,5},{8,10},{10,8},{12,... | collective-permute-start | bytes 4718600 | tf_op jit(solution)/shard_map/ppermute | solution.py:26
  46.3 26.6 %collective-permute-start.9 = (bf16[2,256,1536]{2,1,0:T(8,128)(2,1)}, bf16[2,256,1536]{2,1,0:T(8,128)(2,1)}, u32[]{:S(2)}, u32[]{:S(2)}) collective-permute-start(bf16[2,256,1536]{2,1,0:T(8,128)(2,1)} %fusion.38), channel_id=1, source_target_pairs={{0,2},{2,0},{4,6},{6,4},{1,3},{3,1},{5,7},{7,5},{8,10},{10,8},{12,... | collective-permute-start | bytes 4718600 | tf_op jit(solution)/shard_map/ppermute | solution.py:26
  58.1 17.4 %collective-permute-start = (bf16[2,256,1536]{2,1,0:T(8,128)(2,1)}, bf16[2,256,1536]{2,1,0:T(8,128)(2,1)}, u32[]{:S(2)}, u32[]{:S(2)}) collective-permute-start(bf16[2,256,1536]{2,1,0:T(8,128)(2,1)} %fusion.36), channel_id=1, source_target_pairs={{0,2},{2,0},{4,6},{6,4},{1,3},{3,1},{5,7},{7,5},{8,10},{10,8},{12,... | collective-permute-start | bytes 4718600 | tf_op jit(solution)/shard_map/ppermute | solution.py:26
  58.1 101.3 %collective-permute-start.4 = (bf16[512,3072]{1,0:T(8,128)(2,1)}, bf16[512,3072]{1,0:T(8,128)(2,1)S(1)}, u32[]{:S(2)}, u32[]{:S(2)}) collective-permute-start(bf16[512,3072]{1,0:T(8,128)(2,1)} %bitcast.18), channel_id=1, source_target_pairs={{0,24},{8,0},{16,8},{24,16},{1,25},{9,1},{17,9},{25,17},{2,26},{10... | collective-permute-start | bytes 9437192 | tf_op jit(solution)/shard_map/ppermute | solution.py:13
  65.5 93.9 %collective-permute-start.5 = (f32[1,3072]{1,0:T(1,128)S(1)}, f32[1,3072]{1,0:T(1,128)S(1)}, u32[]{:S(2)}, u32[]{:S(2)}) collective-permute-start(f32[1,3072]{1,0:T(1,128)S(1)} %copy-done.11), channel_id=1, source_target_pairs={{0,24},{8,0},{16,8},{24,16},{1,25},{9,1},{17,9},{25,17},{2,26},{10... | collective-permute-start | bytes 36872 | tf_op jit(solution)/shard_map/ppermute | solution.py:13
  69.1 20.5 %collective-permute-start.13 = (bf16[256,1536]{1,0:T(8,128)(2,1)S(1)}, bf16[256,1536]{1,0:T(8,128)(2,1)S(1)}, u32[]{:S(2)}, u32[]{:S(2)}) collective-permute-start(bf16[256,1536]{1,0:T(8,128)(2,1)S(1)} %fusion.51), channel_id=1, source_target_pairs={{0,4},{2,6},{4,0},{6,2},{1,5},{3,7},{5,1},{7,3},{8,12},{10,14},{12... | collective-permute-start | bytes 2359304 | tf_op jit(solution)/shard_map/ppermute | solution.py:31
  72.9 33.5 %collective-permute-start.7 = (bf16[256,1536]{1,0:T(8,128)(2,1)S(1)}, bf16[256,1536]{1,0:T(8,128)(2,1)S(1)}, u32[]{:S(2)}, u32[]{:S(2)}) collective-permute-start(bf16[256,1536]{1,0:T(8,128)(2,1)S(1)} %fusion.49), channel_id=1, source_target_pairs={{0,4},{2,6},{4,0},{6,2},{1,5},{3,7},{5,1},{7,3},{8,12},{10,14},{12... | collective-permute-start | bytes 2359304 | tf_op jit(solution)/shard_map/ppermute | solution.py:31
  75.6 47.7 %collective-permute-start.10 = (bf16[256,1536]{1,0:T(8,128)(2,1)S(1)}, bf16[256,1536]{1,0:T(8,128)(2,1)S(1)}, u32[]{:S(2)}, u32[]{:S(2)}) collective-permute-start(bf16[256,1536]{1,0:T(8,128)(2,1)S(1)} %fusion.50), channel_id=1, source_target_pairs={{0,4},{2,6},{4,0},{6,2},{1,5},{3,7},{5,1},{7,3},{8,12},{10,14},{12... | collective-permute-start | bytes 2359304 | tf_op jit(solution)/shard_map/ppermute | solution.py:31
  89.6 49.1 %collective-permute-start.1 = (bf16[256,1536]{1,0:T(8,128)(2,1)S(1)}, bf16[256,1536]{1,0:T(8,128)(2,1)S(1)}, u32[]{:S(2)}, u32[]{:S(2)}) collective-permute-start(bf16[256,1536]{1,0:T(8,128)(2,1)S(1)} %fusion.48), channel_id=1, source_target_pairs={{0,4},{2,6},{4,0},{6,2},{1,5},{3,7},{5,1},{7,3},{8,12},{10,14},{12... | collective-permute-start | bytes 2359304 | tf_op jit(solution)/shard_map/ppermute | solution.py:31
  106.4 34.1 %collective-permute-start.14 = (bf16[128,1536]{1,0:T(8,128)(2,1)S(1)}, bf16[128,1536]{1,0:T(8,128)(2,1)S(1)}, u32[]{:S(2)}, u32[]{:S(2)}) collective-permute-start(bf16[128,1536]{1,0:T(8,128)(2,1)S(1)} %dynamic-slice_bitcast_fusion), channel_id=1, source_target_pairs={{0,1},{1,0},{2,3},{3,2},{4,5},{5,4},{6,7},{7,6},{8,9},{9,8},{10,11... | collective-permute-start | bytes 1179656 | tf_op jit(solution)/shard_map/ppermute | solution.py:45
  123.3 30.0 %collective-permute-start.8 = (bf16[128,1536]{1,0:T(8,128)(2,1)S(1)}, bf16[128,1536]{1,0:T(8,128)(2,1)S(1)}, u32[]{:S(2)}, u32[]{:S(2)}) collective-permute-start(bf16[128,1536]{1,0:T(8,128)(2,1)S(1)} %dynamic-slice_bitcast_fusion.2), channel_id=1, source_target_pairs={{0,1},{1,0},{2,3},{3,2},{4,5},{5,4},{6,7},{7,6},{8,9},{9,8},{10,11... | collective-permute-start | bytes 1179656 | tf_op jit(solution)/shard_map/ppermute | solution.py:45
  138.6 12.0 %collective-permute-start.11 = (bf16[128,1536]{1,0:T(8,128)(2,1)S(1)}, bf16[128,1536]{1,0:T(8,128)(2,1)S(1)}, u32[]{:S(2)}, u32[]{:S(2)}) collective-permute-start(bf16[128,1536]{1,0:T(8,128)(2,1)S(1)} %dynamic-slice_bitcast_fusion.1), channel_id=1, source_target_pairs={{0,1},{1,0},{2,3},{3,2},{4,5},{5,4},{6,7},{7,6},{8,9},{9,8},{10,11... | collective-permute-start | bytes 1179656 | tf_op jit(solution)/shard_map/ppermute | solution.py:45
  140.5 16.1 %collective-permute-start.2 = (bf16[128,1536]{1,0:T(8,128)(2,1)S(1)}, bf16[128,1536]{1,0:T(8,128)(2,1)S(1)}, u32[]{:S(2)}, u32[]{:S(2)}) collective-permute-start(bf16[128,1536]{1,0:T(8,128)(2,1)S(1)} %dynamic-slice_bitcast_fusion.3), channel_id=1, source_target_pairs={{0,1},{1,0},{2,3},{3,2},{4,5},{5,4},{6,7},{7,6},{8,9},{9,8},{10,11... | collective-permute-start | bytes 1179656 | tf_op jit(solution)/shard_map/ppermute | solution.py:45
  150.6 67.6 %collective-permute-start.18 = (bf16[128,3072]{1,0:T(8,128)(2,1)}, bf16[128,3072]{1,0:T(8,128)(2,1)}, u32[]{:S(2)}, u32[]{:S(2)}) collective-permute-start(bf16[128,3072]{1,0:T(8,128)(2,1)} %pad_maximum_fusion.3), channel_id=1, source_target_pairs={{0,8},{8,16},{16,24},{24,0},{1,9},{9,17},{17,25},{25,1},{2,10},{10... | collective-permute-start | bytes 2359304 | tf_op jit(solution)/shard_map/ppermute | solution.py:13
  153.3 64.9 %collective-permute-start.17 = (bf16[128,3072]{1,0:T(8,128)(2,1)}, bf16[128,3072]{1,0:T(8,128)(2,1)}, u32[]{:S(2)}, u32[]{:S(2)}) collective-permute-start(bf16[128,3072]{1,0:T(8,128)(2,1)} %pad_maximum_fusion.2), channel_id=1, source_target_pairs={{0,8},{8,16},{16,24},{24,0},{1,9},{9,17},{17,25},{25,1},{2,10},{10... | collective-permute-start | bytes 2359304 | tf_op jit(solution)/shard_map/ppermute | solution.py:13
  156.7 61.5 %collective-permute-start.16 = (bf16[128,3072]{1,0:T(8,128)(2,1)}, bf16[128,3072]{1,0:T(8,128)(2,1)}, u32[]{:S(2)}, u32[]{:S(2)}) collective-permute-start(bf16[128,3072]{1,0:T(8,128)(2,1)} %pad_maximum_fusion.1), channel_id=1, source_target_pairs={{0,8},{8,16},{16,24},{24,0},{1,9},{9,17},{17,25},{25,1},{2,10},{10... | collective-permute-start | bytes 2359304 | tf_op jit(solution)/shard_map/ppermute | solution.py:13
  159.4 58.8 %collective-permute-start.3 = (bf16[128,3072]{1,0:T(8,128)(2,1)}, bf16[128,3072]{1,0:T(8,128)(2,1)}, u32[]{:S(2)}, u32[]{:S(2)}) collective-permute-start(bf16[128,3072]{1,0:T(8,128)(2,1)} %pad_maximum_fusion), channel_id=1, source_target_pairs={{0,8},{8,16},{16,24},{24,0},{1,9},{9,17},{17,25},{25,1},{2,10},{10... | collective-permute-start | bytes 2359304 | tf_op jit(solution)/shard_map/ppermute | solution.py:13
  171.0 47.2 %collective-permute-start.15 = (f32[2,512]{1,0:T(2,128)S(1)}, f32[2,512]{1,0:T(2,128)S(1)}, u32[]{:S(2)}, u32[]{:S(2)}) collective-permute-start(f32[2,512]{1,0:T(2,128)S(1)} %pad_maximum_fusion.4), channel_id=1, source_target_pairs={{0,8},{8,16},{16,24},{24,0},{1,9},{9,17},{17,25},{25,1},{2,10},{10... | collective-permute-start | bytes 12296 | tf_op jit(solution)/shard_map/ppermute | solution.py:13
  176.9 41.3 %copy-start.10 = (f32[1,3072]{1,0:T(1,128)S(1)}, f32[1,3072]{1,0:T(1,128)}, u32[]{:S(2)}) copy-start(f32[1,3072]{1,0:T(1,128)} %param.10) | copy-start | bytes 36868
  176.9 41.3 %copy-start.12 = (f32[1,3072]{1,0:T(1,128)S(1)}, f32[1,3072]{1,0:T(1,128)}, u32[]{:S(2)}) copy-start(f32[1,3072]{1,0:T(1,128)} %param.9) | copy-start | bytes 36868
  (19 other events, 137.2 us)
